TPU v7x, 32 devices: a whole 2x2x4 slice. The times are simulated.
32 devices in a mesh: seq: 4 (over z), fsdp: 8 (over y, x, core).
Axes of the slice: x: 2, y: 2, z: 4, core: 2. Of those that a mesh axis runs over, the one named last changes fastest.
Arguments:
- tokens: bfloat16 [8, 1024, 2048], P('fsdp', 'seq'), may hold values from -6 to 6
- cotangent: bfloat16 [8, 1024, 2048], P('fsdp', 'seq'), may hold values from -6 to 6
- lengths: int32 [8], P('fsdp'), may hold values from 256 to 1024, as said below
- routes: int32 [8, 1024, 8], P('fsdp', 'seq'), may hold values from 0 to 31, as said below
- slots: int32 [8, 1024, 8], P('fsdp', 'seq'), may hold values from -1 to 79, as said below
- w_qkv: bfloat16 [2048, 5120], P(('seq', 'fsdp')), may hold values from -0.125 to 0.125
- w_out: bfloat16 [4096, 2048], P(('seq', 'fsdp')), may hold values from -1.5 to 1.5
- w_router: bfloat16 [2048, 32], P(('seq', 'fsdp')), may hold values from -0.25 to 0.25
- norm_gains: bfloat16 [4352], P(('seq', 'fsdp')), may hold values from 0.25 to 1.75
- w_gate_up: bfloat16 [32, 2048, 1536], P('fsdp', 'seq'), may hold values from -0.125 to 0.125
- w_down: bfloat16 [32, 768, 2048], P('fsdp', None, 'seq'), may hold values from -0.625 to 0.625
Outputs:
- output: bfloat16 [8, 1024, 2048], P('fsdp', 'seq')
- d_input: float32 [8, 1024, 2048], P('fsdp', 'seq')
- grad_qkv: float32 [2048, 5120], P(('seq', 'fsdp'))
- grad_out: float32 [4096, 2048], P(('seq', 'fsdp'))
- grad_router: float32 [2048, 32], P(('seq', 'fsdp'))
- grad_gains: float32 [4352], P(('seq', 'fsdp'))
- grad_gate_up: float32 [32, 2048, 1536], P('fsdp', 'seq')
- grad_down: float32 [32, 768, 2048], P('fsdp', None, 'seq')
Inputs may be any that keep to these rules, and one draw needn't show every extreme that they name: `lengths`: every length is at least a quarter of 1024, and some sequence is 1024 long. `routes`: each token names 8 different experts. Among the valid tokens of one device (aligned blocks of 256 positions of a sequence) that route to one expert, the slots count 0, 1, 2 and so on in order of position while below 80; later ones and all padded slots are -1. In every draw some device sends 80 rows to some expert.
All inputs are finite; a program needn't handle non-finite values.
Results may differ from a plain program's by a relative error of at most 0.019.
Values may be sent and summed in bfloat16 or wider, within the bound.
A program may use at most 384 MiB of HBM per device.

v0:
```python
import jax
import jax.numpy as jnp
from jax import lax
from jax.sharding import PartitionSpec as P

QH = 32
KH = 4
HD = 128
FF = 768
TOPK = 8
EPSILON = 1e-06
THETA = 1000000.0
MASKED = -1e30


def rms_forward(values, gain):
    factor = lax.rsqrt(jnp.mean(values * values, axis=-1, keepdims=True) + EPSILON)
    return (values * factor * gain, factor)


def rms_backward(values, factor, gain, upstream):
    normed = values * factor
    scaled = upstream * gain
    inner = jnp.mean(scaled * normed, axis=-1, keepdims=True)
    grad_values = factor * (scaled - normed * inner)
    grad_gain = jnp.sum((upstream * normed).reshape(-1, values.shape[-1]), axis=0)
    return (grad_values, grad_gain)


def rotate(values, cosine, sine):
    half_dim = values.shape[-1] // 2
    first_half = values[..., :half_dim]
    second_half = values[..., half_dim:]
    return jnp.concatenate(
        [first_half * cosine - second_half * sine, second_half * cosine + first_half * sine],
        axis=-1,
    )


def to_experts(rows, groups):
    shaped = rows.reshape(groups, -1, rows.shape[-1])
    return lax.all_to_all(shaped, "fsdp", split_axis=0, concat_axis=0, tiled=True)


def from_experts(rows):
    returned = lax.all_to_all(rows, "fsdp", split_axis=0, concat_axis=0, tiled=True)
    return returned.reshape(-1, returned.shape[-1])


def expert_weights(w_gate_up, w_down):
    return (
        lax.all_gather(w_gate_up, "seq", axis=1, tiled=True),
        lax.all_gather(w_down, "seq", axis=2, tiled=True),
    )


def per_device(
    tokens, cotangent, lengths, routes, slots, w_qkv, w_out, w_router, norm_gains, w_gate_up, w_down
):
    tok_count = tokens.shape[1]
    width = tokens.shape[2]
    seq_parts = lax.axis_size("seq")
    fsdp_parts = lax.axis_size("fsdp")
    local_experts = w_gate_up.shape[0]
    heads_local = QH // seq_parts
    kv_local = KH // seq_parts
    group_size = QH // KH
    seq_total = tok_count * seq_parts
    layer_inputs = tokens[0].astype(jnp.float32)
    full_qkv, full_out, full_router, full_gains = (
        lax.all_gather(w_qkv, ("seq", "fsdp"), axis=0, tiled=True),
        lax.all_gather(w_out, ("seq", "fsdp"), axis=0, tiled=True),
        lax.all_gather(w_router, ("seq", "fsdp"), axis=0, tiled=True),
        lax.all_gather(norm_gains, ("seq", "fsdp"), axis=0, tiled=True),
    )
    gain_values = full_gains.astype(jnp.float32)
    gain_attn = gain_values[:width]
    gain_ffn = gain_values[width : 2 * width]
    gain_query = gain_values[2 * width : 2 * width + HD]
    gain_key = gain_values[2 * width + HD :]
    expert_count = full_router.shape[1]
    capacity = tok_count * TOPK * 5 // (4 * expert_count)
    total_slots = expert_count * capacity
    attn_normed, attn_factor = rms_forward(layer_inputs, gain_attn)
    attention_reduced = attn_normed.astype(jnp.bfloat16)
    projected_rows = jnp.dot(attention_reduced, full_qkv, preferred_element_type=jnp.float32)
    query_raw = projected_rows[:, : QH * HD].reshape(tok_count, QH, HD)
    key_raw = projected_rows[:, QH * HD : (QH + KH) * HD].reshape(tok_count, KH, HD)
    value_raw = projected_rows[:, (QH + KH) * HD :].reshape(tok_count, KH, HD)
    query_normed, query_factor = rms_forward(query_raw, gain_query)
    key_normed, key_factor = rms_forward(key_raw, gain_key)
    positions = lax.axis_index("seq") * tok_count + jnp.arange(tok_count, dtype=jnp.int32)
    frequency = THETA ** (-jnp.arange(HD // 2, dtype=jnp.float32) / (HD // 2))
    angles = positions.astype(jnp.float32)[:, None] * frequency[None, :]
    cosine = jnp.cos(angles)[:, None, :]
    sine = jnp.sin(angles)[:, None, :]
    query_send = (
        rotate(query_normed, cosine, sine)
        .astype(jnp.bfloat16)
        .reshape(tok_count, seq_parts, heads_local, HD)
    )
    kv_stack = jnp.stack([rotate(key_normed, cosine, sine), value_raw], axis=2)
    kv_send = kv_stack.astype(jnp.bfloat16)
    query_heads, kv_heads = (
        lax.all_to_all(query_send, "seq", split_axis=1, concat_axis=0, tiled=True),
        lax.all_to_all(kv_send, "seq", split_axis=1, concat_axis=0, tiled=True),
    )
    key_all = kv_heads[:, :, 0]
    value_all = kv_heads[:, :, 1]
    seq_length = lengths[0]
    block = min(512, seq_total)
    block_count = seq_total // block
    scale = HD ** (-0.5)
    query_blocks = query_heads.reshape(block_count, block, kv_local, group_size, HD)
    starts = jnp.arange(block_count, dtype=jnp.int32) * block
    key_index = jnp.arange(seq_total, dtype=jnp.int32)

    def block_scores(start, query_block):
        scores = (
            jnp.einsum("qkgd,pkd->kgqp", query_block, key_all, preferred_element_type=jnp.float32)
            * scale
        )
        query_index = start + jnp.arange(block, dtype=jnp.int32)
        allowed = (key_index[None, :] <= query_index[:, None]) & (key_index[None, :] < seq_length)
        return jnp.where(allowed, scores, MASKED)

    def attend_block(pieces):
        start, query_block = pieces
        scores = block_scores(start, query_block)
        peak = jnp.max(scores, axis=-1, keepdims=True)
        weights = jnp.exp(scores - peak)
        totals = jnp.sum(weights, axis=-1, keepdims=True)
        probs = weights / totals
        mixed_tokens = jnp.einsum(
            "kgqp,pkd->qkgd",
            probs.astype(jnp.bfloat16),
            value_all,
            preferred_element_type=jnp.float32,
        )
        return (mixed_tokens.astype(jnp.bfloat16), (peak + jnp.log(totals))[..., 0])

    attn_blocks, log_totals = lax.map(attend_block, (starts, query_blocks))
    attn_send = attn_blocks.reshape(seq_total, 1, heads_local, HD)
    attn_tokens = lax.all_to_all(attn_send, "seq", split_axis=0, concat_axis=1, tiled=True).reshape(
        tok_count, QH * HD
    )
    residual_stream = layer_inputs + jnp.dot(
        attn_tokens, full_out, preferred_element_type=jnp.float32
    )
    ffn_normed, ffn_factor = rms_forward(residual_stream, gain_ffn)
    feedforward_reduced = ffn_normed.astype(jnp.bfloat16)
    router_scores = jnp.dot(feedforward_reduced, full_router, preferred_element_type=jnp.float32)
    route_rows = routes[0]
    slot_rows = slots[0]
    picked = route_rows[:, :, None] == jnp.arange(expert_count, dtype=jnp.int32)[None, None, :]
    selected = jnp.sum(jnp.where(picked, router_scores[:, None, :], 0.0), axis=-1)
    gate_prob = jax.nn.softmax(selected, axis=-1)
    flat_pos = jnp.where(slot_rows >= 0, route_rows * capacity + slot_rows, total_slots).reshape(-1)
    owner = (
        jnp.full((total_slots,), tok_count * TOPK, jnp.int32)
        .at[flat_pos]
        .set(jnp.arange(tok_count * TOPK, dtype=jnp.int32), mode="drop")
    )
    send_rows = jnp.take(feedforward_reduced, owner // TOPK, axis=0, mode="fill", fill_value=0)
    received = to_experts(send_rows, fsdp_parts)
    expert_rows = received.reshape(fsdp_parts, local_experts, capacity, width)
    full_gate_up, full_down = expert_weights(w_gate_up, w_down)
    gate_up = jnp.einsum(
        "sjcd,jdf->sjcf", expert_rows, full_gate_up, preferred_element_type=jnp.float32
    )
    gate_part = gate_up[..., :FF]
    up_part = gate_up[..., FF:]
    hidden_low = (jax.nn.silu(gate_part) * up_part).astype(jnp.bfloat16)
    expert_out = jnp.einsum(
        "sjch,jhd->sjcd", hidden_low, full_down, preferred_element_type=jnp.float32
    ).astype(jnp.bfloat16)
    returned = from_experts(expert_out.reshape(fsdp_parts, local_experts * capacity, width))
    token_out = jnp.take(returned, flat_pos, axis=0, mode="fill", fill_value=0).reshape(
        tok_count, TOPK, width
    )
    token_wide = token_out.astype(jnp.float32)
    moe_out = jnp.sum(gate_prob[:, :, None] * token_wide, axis=1)
    valid = positions < seq_length
    final = jnp.where(valid[:, None], residual_stream + moe_out, 0.0)
    grad_final = jnp.where(valid[:, None], cotangent[0].astype(jnp.float32), 0.0)
    grad_prob = jnp.sum(token_wide * grad_final[:, None, :], axis=-1)
    grad_selected = gate_prob * (grad_prob - jnp.sum(gate_prob * grad_prob, axis=-1, keepdims=True))
    grad_logits = jnp.sum(jnp.where(picked, grad_selected[:, :, None], 0.0), axis=1).astype(
        jnp.bfloat16
    )
    grad_token_out = (
        (gate_prob[:, :, None] * grad_final[:, None, :])
        .astype(jnp.bfloat16)
        .reshape(tok_count * TOPK, width)
    )
    grad_send = jnp.take(grad_token_out, owner, axis=0, mode="fill", fill_value=0)
    grad_rows = to_experts(grad_send, fsdp_parts).reshape(
        fsdp_parts, local_experts, capacity, width
    )
    again_gate_up, again_down = expert_weights(w_gate_up, w_down)
    grad_hidden_low = jnp.einsum(
        "sjcd,jhd->sjch", grad_rows, again_down, preferred_element_type=jnp.float32
    ).astype(jnp.bfloat16)
    grad_hidden = lax.optimization_barrier(grad_hidden_low).astype(jnp.float32)
    sigmoid_gate = jax.nn.sigmoid(gate_part)
    grad_gate = grad_hidden * up_part * sigmoid_gate * (1.0 + gate_part * (1.0 - sigmoid_gate))
    grad_up = grad_hidden * gate_part * sigmoid_gate
    grad_gu_low = jnp.concatenate([grad_gate, grad_up], axis=-1).astype(jnp.bfloat16)
    grad_expert_rows = jnp.einsum(
        "sjcf,jdf->sjcd", grad_gu_low, again_gate_up, preferred_element_type=jnp.float32
    ).astype(jnp.bfloat16)
    grad_back = from_experts(grad_expert_rows.reshape(fsdp_parts, local_experts * capacity, width))
    partial_gate_up = jnp.einsum(
        "sjcd,sjcf->jdf", expert_rows, grad_gu_low, preferred_element_type=jnp.float32
    )
    partial_down = jnp.einsum(
        "sjch,sjcd->jhd", hidden_low, grad_rows, preferred_element_type=jnp.float32
    )
    grad_gate_up, grad_down = (
        lax.psum_scatter(
            partial_gate_up.astype(jnp.bfloat16), "seq", scatter_dimension=1, tiled=True
        ).astype(jnp.float32),
        lax.psum_scatter(
            partial_down.astype(jnp.bfloat16), "seq", scatter_dimension=2, tiled=True
        ).astype(jnp.float32),
    )
    grad_from_rows = jnp.sum(
        jnp.take(grad_back, flat_pos, axis=0, mode="fill", fill_value=0)
        .reshape(tok_count, TOPK, width)
        .astype(jnp.float32),
        axis=1,
    )
    grad_ffn = grad_from_rows + jnp.einsum(
        "te,de->td", grad_logits, full_router, preferred_element_type=jnp.float32
    )
    grad_router_local = jnp.einsum(
        "td,te->de", feedforward_reduced, grad_logits, preferred_element_type=jnp.float32
    )
    grad_res_norm, grad_gain_ffn = rms_backward(residual_stream, ffn_factor, gain_ffn, grad_ffn)
    grad_residual = grad_final + grad_res_norm
    grad_attn_low = grad_residual.astype(jnp.bfloat16)
    grad_out_local = jnp.einsum(
        "te,td->ed", attn_tokens, grad_attn_low, preferred_element_type=jnp.float32
    )
    grad_attn_tokens = jnp.einsum(
        "td,ed->te", grad_attn_low, full_out, preferred_element_type=jnp.float32
    ).astype(jnp.bfloat16)
    grad_heads_send = grad_attn_tokens.reshape(tok_count, seq_parts, heads_local, HD)
    grad_attn_heads = lax.all_to_all(
        grad_heads_send, "seq", split_axis=1, concat_axis=0, tiled=True
    ).reshape(block_count, block, kv_local, group_size, HD)

    def attend_back(carry, pieces):
        start, query_block, grad_block, log_block = pieces
        scores = block_scores(start, query_block)
        probs = jnp.exp(scores - log_block[..., None])
        grad_probs = jnp.einsum(
            "qkgd,pkd->kgqp", grad_block, value_all, preferred_element_type=jnp.float32
        )
        inner = jnp.sum(probs * grad_probs, axis=-1, keepdims=True)
        grad_scores = (probs * (grad_probs - inner)).astype(jnp.bfloat16)
        grad_query = (
            jnp.einsum("kgqp,pkd->qkgd", grad_scores, key_all, preferred_element_type=jnp.float32)
            * scale
        )
        grad_key = (
            carry[0]
            + jnp.einsum(
                "kgqp,qkgd->pkd", grad_scores, query_block, preferred_element_type=jnp.float32
            )
            * scale
        )
        grad_value = carry[1] + jnp.einsum(
            "kgqp,qkgd->pkd",
            probs.astype(jnp.bfloat16),
            grad_block,
            preferred_element_type=jnp.float32,
        )
        return ((grad_key, grad_value), grad_query.astype(jnp.bfloat16))

    zeros_kv = jnp.zeros((seq_total, kv_local, HD), jnp.float32)
    kv_grads, grad_query_blocks = lax.scan(
        attend_back, (zeros_kv, zeros_kv), (starts, query_blocks, grad_attn_heads, log_totals)
    )
    grad_query_send = grad_query_blocks.reshape(seq_total, 1, heads_local, HD)
    grad_kv_send = jnp.stack([kv_grads[0], kv_grads[1]], axis=2).astype(jnp.bfloat16)
    grad_query_tok, grad_kv_tok = (
        lax.all_to_all(grad_query_send, "seq", split_axis=0, concat_axis=1, tiled=True),
        lax.all_to_all(grad_kv_send, "seq", split_axis=0, concat_axis=1, tiled=True),
    )
    grad_query_rot = grad_query_tok.reshape(tok_count, QH, HD).astype(jnp.float32)
    grad_kv_pair = grad_kv_tok.astype(jnp.float32)
    grad_query_norm = rotate(grad_query_rot, cosine, -sine)
    grad_key_norm = rotate(grad_kv_pair[:, :, 0], cosine, -sine)
    grad_query_raw, grad_gain_query = rms_backward(
        query_raw, query_factor, gain_query, grad_query_norm
    )
    grad_key_raw, grad_gain_key = rms_backward(key_raw, key_factor, gain_key, grad_key_norm)
    grad_projected = jnp.concatenate(
        [
            grad_query_raw.reshape(tok_count, -1),
            grad_key_raw.reshape(tok_count, -1),
            grad_kv_pair[:, :, 1].reshape(tok_count, -1),
        ],
        axis=-1,
    ).astype(jnp.bfloat16)
    grad_qkv_local = jnp.einsum(
        "td,te->de", attention_reduced, grad_projected, preferred_element_type=jnp.float32
    )
    grad_attn_norm = jnp.einsum(
        "te,de->td", grad_projected, full_qkv, preferred_element_type=jnp.float32
    )
    grad_in_norm, grad_gain_attn = rms_backward(
        layer_inputs, attn_factor, gain_attn, grad_attn_norm
    )
    grad_inputs = grad_residual + grad_in_norm
    grad_gain_local = jnp.concatenate(
        [grad_gain_attn, grad_gain_ffn, grad_gain_query, grad_gain_key]
    )
    grad_qkv, grad_out, grad_router, grad_gains = (
        lax.psum_scatter(grad_qkv_local, ("seq", "fsdp"), scatter_dimension=0, tiled=True),
        lax.psum_scatter(grad_out_local, ("seq", "fsdp"), scatter_dimension=0, tiled=True),
        lax.psum_scatter(grad_router_local, ("seq", "fsdp"), scatter_dimension=0, tiled=True),
        lax.psum_scatter(grad_gain_local, ("seq", "fsdp"), scatter_dimension=0, tiled=True),
    )
    return (
        final.astype(jnp.bfloat16)[None],
        grad_inputs[None],
        grad_qkv,
        grad_out,
        grad_router,
        grad_gains,
        grad_gate_up,
        grad_down,
    )


def solution(mesh):
    in_specs = (
        P("fsdp", "seq", None),
        P("fsdp", "seq", None),
        P("fsdp"),
        P("fsdp", "seq", None),
        P("fsdp", "seq", None),
        P(("seq", "fsdp"), None),
        P(("seq", "fsdp"), None),
        P(("seq", "fsdp"), None),
        P(("seq", "fsdp")),
        P("fsdp", "seq", None),
        P("fsdp", None, "seq"),
    )
    out_specs = (
        P("fsdp", "seq", None),
        P("fsdp", "seq", None),
        P(("seq", "fsdp"), None),
        P(("seq", "fsdp"), None),
        P(("seq", "fsdp"), None),
        P(("seq", "fsdp")),
        P("fsdp", "seq", None),
        P("fsdp", None, "seq"),
    )
    return jax.shard_map(
        per_device, mesh=mesh, in_specs=in_specs, out_specs=out_specs, check_vma=False
    )
```

profile of v0, /device:TPU:1, one launch (start us, length us, event | category | flops | bytes accessed | tf_op | source)
XLA Modules:
  0.0 2935.8 jit_solution(3015769868315914340)
XLA Ops:
  10.8 43.2 %all-reduce = bf16[4352]{0:T(1024)(128)(2,1)S(1)} all-reduce(bf16[4352]{0:T(1024)(128)(2,1)S(1)} %dynamic-update-slice), channel_id=1, replica_groups=mesh['seq'=4,'fsdp'=8] {'seq','fsdp'}, use_global_device_ids=true, to_apply=%add | all-reduce | flops 4352 | bytes 17408
  55.0 93.7 %all-gather.6.cloned.1.call-done = bf16[2048,5120]{1,0:T(8,128)(2,1)} async-done(((bf16[64,5120]{1,0:T(8,128)(2,1)}), bf16[2048,5120]{1,0:T(8,128)(2,1)}) %all-gather.6.cloned.1.call-update) | async-done | bytes 20971536 | tf_op jit(solution)/shard_map/all_gather | solution.py:71
  193.0 87.5 %all-to-all-done = bf16[256,4,8,128]{0,3,2,1:T(8,128)(2,1)S(1)} async-done(((bf16[256,4,8,128]{0,3,2,1:T(8,128)(2,1)}), bf16[256,4,8,128]{0,3,2,1:T(8,128)(2,1)S(1)}, u32[]{:S(2)}, u32[]{:S(2)}) %all-to-all-start) | async-done | bytes 2097184 | tf_op jit(solution)/shard_map/all_to_all | solution.py:105
  286.6 33.9 %while.30 = (s32[]{:T(128)}, bf16[2,512,1,8,128]{4,3,1,0,2:T(8,128)(2,1)}, f32[2,1,8,512]{3,2,1,0:T(8,128)S(1)}, s32[2]{0:T(128)S(1)}, s32[]{:T(128)}, /*index=5...) while((s32[]{:T(128)}, ...), condition=%wide.region_6.7_spmd.clone.clone, body=%wide.region_3.6_spmd.clone.clone.sunk | while | flops 2199385600 | bytes 57285240 | solution.py:142
  339.3 99.5 %all-to-all-done.2 = bf16[1024,1,8,128]{3,2,1,0:T(8,128)(2,1)} async-done(((bf16[1024,1,8,128]{3,2,1,0:T(8,128)(2,1)}), bf16[1024,1,8,128]{3,2,1,0:T(8,128)(2,1)}, u32[]{:S(2)}, u32[]{:S(2)}) %all-to-all-start.2) | async-done | bytes 2097184 | tf_op jit(solution)/shard_map/all_to_all | solution.py:144
  480.3 290.4 %all-gather.10.cloned.1.call-done = bf16[4,2048,1536]{2,1,0:T(8,128)(2,1)} async-done(((bf16[4,512,1536]{2,1,0:T(8,128)(2,1)}), bf16[4,2048,1536]{2,1,0:T(8,128)(2,1)}) %all-gather.10.cloned.1.call-update) | async-done | bytes 25165840 | tf_op jit(solution)/shard_map/all_gather | solution.py:52
  770.7 25.7 fusion.75
  804.5 183.9 %all-gather.12.cloned.1.call-done = bf16[4,768,2048]{2,1,0:T(8,128)(2,1)} async-done(((bf16[4,768,512]{2,1,0:T(8,128)(2,1)}), bf16[4,768,2048]{2,1,0:T(8,128)(2,1)}) %all-gather.12.cloned.1.call-update) | async-done | bytes 12582928 | tf_op jit(solution)/shard_map/all_gather | solution.py:53
  1021.0 145.7 %all-gather = bf16[32,64,32]{1,2,0:T(8,128)(2,1)S(1)} all-gather(bf16[1,64,32]{1,2,0:T(8,128)(2,1)S(1)} %bitcast.454), channel_id=1, replica_groups=mesh['seq'=4,'fsdp'=8] {'seq','fsdp'}, dimensions={0}, use_global_device_ids=true | all-gather | bytes 135168 | tf_op jit(solution)/shard_map/all_gather | solution.py:73
  1169.3 21.6 gather_fusion.2
  1201.4 24.6 gather_fusion.1
  1243.5 121.0 %all-to-all-done.5 = bf16[8,320,2048]{2,1,0:T(8,128)(2,1)} async-done(((bf16[8,320,2048]{2,1,0:T(8,128)(2,1)}), bf16[8,320,2048]{2,1,0:T(8,128)(2,1)}, u32[]{:S(2)}, u32[]{:S(2)}) %all-to-all-start.5) | async-done | bytes 10485792 | tf_op jit(solution)/shard_map/all_to_all | solution.py:42
  1408.6 27.0 bitcast_convert_fusion
  1435.8 23.5 convert_bitcast_fusion.1
  1469.4 125.6 %all_to_all.101 = bf16[8,320,2048]{2,1,0:T(8,128)(2,1)} all-to-all(bf16[8,320,2048]{2,1,0:T(8,128)(2,1)} %bitcast.424), channel_id=1, replica_groups=mesh['seq'=4,'fsdp'=8] {'fsdp'}, dimensions={0} | all-to-all | bytes 20971520 | tf_op jit(solution)/shard_map/all_to_all | solution.py:46
  1595.0 21.7 gather_fusion.3
  1650.8 18.6 fusion.106
  1677.0 104.5 %all-to-all-done.7 = bf16[256,4,8,128]{3,2,0,1:T(8,128)(2,1)S(1)} async-done(((bf16[256,4,8,128]{3,2,0,1:T(8,128)(2,1)}), bf16[256,4,8,128]{3,2,0,1:T(8,128)(2,1)S(1)}, u32[]{:S(2)}, u32[]{:S(2)}) %all-to-all-start.7) | async-done | bytes 2097184 | tf_op jit(solution)/shard_map/all_to_all | solution.py:249
  1783.1 91.1 %while.31 = (s32[]{:T(128)}, f32[1024,1,128]{0,2,1:T(8,128)}, f32[1024,1,128]{0,2,1:T(8,128)}, bf16[2,512,1,8,128]{4,3,1,0,2:T(8,128)(2,1)}, bf16[2,512,1,8,128]...) while((s32[]{:T(128)}, f32[1024,1,128]{0,2,1:T(8,128)}, ...), condition=%wide.region_20.22_spmd.clone.clone, body=%wide.region_18.21_spmd.clone.clone.sunk | while | flops 5409207808 | bytes 199187792 | solution.py:282
  1877.3 30.9 %all_to_all.102 = bf16[1024,1,2,128]{3,2,1,0:T(2,128)(2,1)S(1)} all-to-all(bf16[1024,1,2,128]{3,2,1,0:T(2,128)(2,1)S(1)} %copy.408), channel_id=1, replica_groups=mesh['seq'=4,'fsdp'=8] {'seq'}, dimensions={0} | all-to-all | bytes 1048576 | tf_op jit(solution)/shard_map/all_to_all | solution.py:289
  1925.4 86.4 %all-to-all-done.8 = bf16[1024,1,8,128]{3,2,1,0:T(8,128)(2,1)S(1)} async-done(((bf16[1024,1,8,128]{3,2,1,0:T(8,128)(2,1)}), bf16[1024,1,8,128]{3,2,1,0:T(8,128)(2,1)S(1)}, u32[]{:S(2)}, u32[]{:S(2)}) %all-to-all-start.8) | async-done | bytes 2097184 | tf_op jit(solution)/shard_map/all_to_all | solution.py:288
  2111.1 66.4 %all-reduce.1 = f32[4352]{0:T(1024)S(1)} all-reduce(f32[4352]{0:T(1024)S(1)} %pad_maximum_fusion.9), channel_id=5, replica_groups=mesh['seq'=4,'fsdp'=8] {'seq','fsdp'}, use_global_device_ids=true, to_apply=%region_31.33.clone | all-reduce | flops 4352 | bytes 34816
  2196.6 278.3 %reduce-scatter.10.cloned.1.call-done = f32[128,2048]{1,0:T(8,128)} async-done(((f32[4096,2048]{1,0:T(8,128)}), f32[128,2048]{1,0:T(8,128)}) %reduce-scatter.10.cloned.1.call-update) | async-done | bytes 1048592 | tf_op jit(solution)/shard_map/reduce_scatter | solution.py:322
  2474.9 454.0 %reduce-scatter.8.cloned.1.call-done = f32[64,5120]{1,0:T(8,128)} async-done(((f32[2048,5120]{1,0:T(8,128)}), f32[64,5120]{1,0:T(8,128)}) %reduce-scatter.8.cloned.1.call-update) | async-done | bytes 1310736 | tf_op jit(solution)/shard_map/reduce_scatter | solution.py:321
  (386 shorter events, 545.2 us)
Async XLA Ops:
  7.2 141.6 %all-gather.6.cloned.1.call-start = ((), (), s32[]{:S(2)}) async-start(), calls=%async_computation.15 | async-start | bytes 21626880 | tf_op jit(solution)/shard_map/all_gather | solution.py:71
  7.9 435.2 %all-gather.8.cloned.1.call-start = ((), (), s32[]{:S(2)}) async-start(), calls=%async_computation.16 | async-start | bytes 17301504 | tf_op jit(solution)/shard_map/all_gather | solution.py:72
  8.7 762.0 %all-gather.10.cloned.1.call-start = ((), (), s32[]{:S(2)}) async-start(), calls=%async_computation.17 | async-start | bytes 31457280 | tf_op jit(solution)/shard_map/all_gather | solution.py:52
  10.4 175.6 %copy-start.32 = (f32[256,64]{0,1:T(8,128)}, f32[256,64]{0,1:T(8,128)S(1)}, u32[]{:S(2)}) copy-start(f32[256,64]{0,1:T(8,128)S(1)} %get-tuple-element.494) | copy-start | bytes 196612
  10.5 151.7 %copy-start.28 = (f32[256,64]{1,0:T(8,128)}, f32[256,64]{1,0:T(8,128)S(1)}, u32[]{:S(2)}) copy-start(f32[256,64]{1,0:T(8,128)S(1)} %copy.374) | copy-start | bytes 196612
  54.4 128.6 %copy-start.63 = (f32[128]{0:T(128)}, f32[128]{0:T(128)S(1)}, u32[]{:S(2)}) copy-start(f32[128]{0:T(128)S(1)} %get-tuple-element.491) | copy-start | bytes 1540
  163.4 24.7 all-to-all-start.1
  188.1 92.4 %all-to-all-start = ((bf16[256,4,8,128]{0,3,2,1:T(8,128)(2,1)}), bf16[256,4,8,128]{0,3,2,1:T(8,128)(2,1)S(1)}, u32[]{:S(2)}, u32[]{:S(2)}) async-start(bf16[256,4,8,128]{0,3,2,1:T(8,128)(2,1)} %pad_maximum_fusion.3), calls=%async_computation | async-start | bytes 4194304 | tf_op jit(solution)/shard_map/all_to_all | solution.py:105
  320.5 122.6 %copy-start.1 = (bf16[2,512,1,8,128]{4,1,3,2,0:T(8,128)(2,1)}, bf16[2,512,1,8,128]{4,1,3,2,0:T(8,128)(2,1)S(1)}, u32[]{:S(2)}) copy-start(bf16[2,512,1,8,128]{4,1,3,2,0:T(8,128)(2,1)S(1)} %get-tuple-element.702) | copy-start | bytes 6291460
  320.5 122.6 %copy-start.6 = (bf16[1024,1,128]{2,0,1:T(8,128)(2,1)}, bf16[1024,1,128]{2,0,1:T(8,128)(2,1)S(1)}, u32[]{:S(2)}) copy-start(bf16[1024,1,128]{2,0,1:T(8,128)(2,1)S(1)} %get-tuple-element.709) | copy-start | bytes 786436
  321.2 117.6 %all-to-all-start.2 = ((bf16[1024,1,8,128]{3,2,1,0:T(8,128)(2,1)}), bf16[1024,1,8,128]{3,2,1,0:T(8,128)(2,1)}, u32[]{:S(2)}, u32[]{:S(2)}) async-start(bf16[1024,1,8,128]{3,2,1,0:T(8,128)(2,1)} %bitcast.17), calls=%async_computation.2 | async-start | bytes 4194304 | tf_op jit(solution)/shard_map/all_to_all | solution.py:144
  325.7 662.8 %all-gather.12.cloned.1.call-start = ((), (), s32[]{:S(2)}) async-start(), calls=%async_computation.18 | async-start | bytes 15728640 | tf_op jit(solution)/shard_map/all_gather | solution.py:53
  474.4 296.4 %all-to-all-start.3 = ((bf16[8,320,2048]{2,1,0:T(8,128)(2,1)}), bf16[8,320,2048]{2,1,0:T(8,128)(2,1)}, u32[]{:S(2)}, u32[]{:S(2)}) async-start(bf16[8,320,2048]{2,1,0:T(8,128)(2,1)} %broadcast_select_fusion.1), calls=%async_computation.3 | async-start | bytes 20971520 | tf_op jit(solution)/shard_map/all_to_all | solution.py:42
  1014.6 154.7 %all-to-all-start.4 = ((bf16[8,320,2048]{2,1,0:T(8,128)(2,1)}), bf16[8,320,2048]{2,1,0:T(8,128)(2,1)}, u32[]{:S(2)}, u32[]{:S(2)}) async-start(bf16[8,320,2048]{2,1,0:T(8,128)(2,1)} %bitcast.421), calls=%async_computation.4 | async-start | bytes 20971520 | tf_op jit(solution)/shard_map/all_to_all | solution.py:46
  1020.2 148.9 %copy-start.50 = (s32[1,256,8]{1,2,0:T(8,128)S(1)}, s32[1,256,8]{1,2,0:T(8,128)}, u32[]{:S(2)}) copy-start(s32[1,256,8]{1,2,0:T(8,128)} %param.20) | copy-start | bytes 24580
  1236.0 128.5 %all-to-all-start.5 = ((bf16[8,320,2048]{2,1,0:T(8,128)(2,1)}), bf16[8,320,2048]{2,1,0:T(8,128)(2,1)}, u32[]{:S(2)}, u32[]{:S(2)}) async-start(bf16[8,320,2048]{2,1,0:T(8,128)(2,1)} %broadcast_select_fusion), calls=%async_computation.5 | async-start | bytes 20971520 | tf_op jit(solution)/shard_map/all_to_all | solution.py:42
  1241.2 836.0 %reduce-scatter.16.cloned.1.call-start = ((), (), s32[]{:S(2)}) async-start(), calls=%async_computation.23 | async-start | bytes 1081344
  1243.4 938.1 %reduce-scatter.14.cloned.1.call-start = ((), (), s32[]{:S(2)}) async-start(), calls=%async_computation.22 | async-start | bytes 15728640 | tf_op jit(solution)/shard_map/reduce_scatter | solution.py:223
  1381.2 805.9 %reduce-scatter.12.cloned.1.call-start = ((), (), s32[]{:S(2)}) async-start(), calls=%async_computation.21 | async-start | bytes 31457280 | tf_op jit(solution)/shard_map/reduce_scatter | solution.py:220
  1435.6 1039.3 %reduce-scatter.10.cloned.1.call-start = ((), (), s32[]{:S(2)}) async-start(), calls=%async_computation.20 | async-start | bytes 34603008 | tf_op jit(solution)/shard_map/reduce_scatter | solution.py:322
  1469.4 125.6 %copy-start.48 = (s32[2048]{0:T(1024)S(1)}, s32[2048]{0:T(1024)}, u32[]{:S(2)}) copy-start(s32[2048]{0:T(1024)} %copy-done.47) | copy-start | bytes 24580
  1673.2 108.3 %all-to-all-start.7 = ((bf16[256,4,8,128]{3,2,0,1:T(8,128)(2,1)}), bf16[256,4,8,128]{3,2,0,1:T(8,128)(2,1)S(1)}, u32[]{:S(2)}, u32[]{:S(2)}) async-start(bf16[256,4,8,128]{3,2,0,1:T(8,128)(2,1)} %copy.394), calls=%async_computation.7 | async-start | bytes 4194304 | tf_op jit(solution)/shard_map/all_to_all | solution.py:249
  1908.2 103.7 %all-to-all-start.8 = ((bf16[1024,1,8,128]{3,2,1,0:T(8,128)(2,1)}), bf16[1024,1,8,128]{3,2,1,0:T(8,128)(2,1)S(1)}, u32[]{:S(2)}, u32[]{:S(2)}) async-start(bf16[1024,1,8,128]{3,2,1,0:T(8,128)(2,1)} %bitcast.52), calls=%async_computation.8 | async-start | bytes 4194304 | tf_op jit(solution)/shard_map/all_to_all | solution.py:288
  1911.8 1017.0 %reduce-scatter.8.cloned.1.call-start = ((), (), s32[]{:S(2)}) async-start(), calls=%async_computation.19 | async-start | bytes 43253760 | tf_op jit(solution)/shard_map/reduce_scatter | solution.py:321
  (73 other events, 1281.6 us)
Sparse Core Ops, SparseCore 0:
  10.9 137.8 all-gather.5
  151.6 149.6 all-gather.7
  302.9 467.8 all-gather.9
  772.1 216.3 all-gather.11
  1243.9 132.1 reduce-scatter.15
  1381.3 211.5 reduce-scatter.13
  1595.3 505.6 reduce-scatter.11
  2103.8 371.0 reduce-scatter.9
  2477.8 451.0 reduce-scatter.7
where the time goes:
time: 2950 us; the launch traced here: 2940 us
  waiting for transfers between devices  1800 us (61%)
  blocking collectives  412 us (14%)
  matrix products  288 us (10%)
  local copies, waits for them, and re-layouts  220 us (7%)
  other arithmetic  159 us (5%)
  starting transfers between devices  37.8 us (1%)
    reduce_scatter x1, waiting for transfers between devices, per_device(): lax.psum_scatter(grad_qkv_local, ('seq', 'fsdp'), scatter_dimension=0, ti...  454 us
    all_gather x1, waiting for transfers between devices, expert_weights(): lax.all_gather(w_gate_up, 'seq', axis=1, tiled=True)  290 us
    reduce_scatter x1, waiting for transfers between devices, per_device(): lax.psum_scatter(grad_out_local, ('seq', 'fsdp'), scatter_dimension=0, ti...  278 us
    all_gather x1, waiting for transfers between devices, expert_weights(): lax.all_gather(w_down, 'seq', axis=2, tiled=True)  184 us
    all_gather x1, blocking collectives, per_device(): lax.all_gather(w_router, ('seq', 'fsdp'), axis=0, tiled=True)  146 us
    all_to_all x1, blocking collectives, from_experts(): lax.all_to_all(rows, 'fsdp', split_axis=0, concat_axis=0, tiled=True)  126 us
    all_to_all x2, waiting for transfers between devices, to_experts(): lax.all_to_all(shaped, 'fsdp', split_axis=0, concat_axis=0, tiled=True)  121 us
    unnamed x2, blocking collectives  110 us
  transfers between devices with their start and end apart: 17, of which 10 were waited for; matrix products, arithmetic and copies ran while one was open for 19% of the time, Pallas kernels for 0%

commit v1 on v0

--- a/solution.py
+++ b/solution.py
@@ -1,3 +1,4 @@
+import functools
 import jax
 import jax.numpy as jnp
 from jax import lax
@@ -11,6 +12,41 @@
 EPSILON = 1e-06
 THETA = 1000000.0
 MASKED = -1e30
+
+
+def core_guide(q_in, dim_i, state):
+    y_new, later = (q_in.shape[:dim_i], q_in.shape[dim_i + 1 :])
+    ready = q_in.reshape(*y_new, state, -1, *later)
+    e_next = jnp.moveaxis(ready, dim_i, 0)
+    return e_next
+
+
+def stocks_number(block_in, pos_dim):
+    block_in = jnp.moveaxis(block_in, 0, pos_dim)
+    extra = block_in.shape
+    fresh = block_in.reshape(
+        *extra[:pos_dim], extra[pos_dim] * extra[pos_dim + 1], *extra[pos_dim + 2 :]
+    )
+    return fresh
+
+
+def series_all_step_on(payload, axis_key, vec, local_array):
+    mid_arr = jax.lax.axis_size(axis_key)
+    w_next = jax.lax.axis_index(axis_key)
+    out_arr, v_next = (mid_arr, w_next)
+    near = core_guide(payload, vec, out_arr)
+    stack_in = [near[v_next]]
+    for kk in range(1, out_arr):
+        after = near[(v_next + kk) % out_arr]
+        r2 = jax.lax.ppermute(after, axis_key, [(m, (m + kk) % out_arr) for m in range(out_arr)])
+        stack_in.append(r2)
+    step_out = jnp.stack(stack_in)
+    near = step_out[(v_next - jnp.arange(out_arr)) % out_arr]
+    arr_next = stocks_number(near, local_array)
+    return arr_next
+
+
+register_the_sides = functools.partial(series_all_step_on, axis_key="seq", vec=0, local_array=1)
 
 
 def rms_forward(values, gain):
@@ -285,7 +321,7 @@
     grad_query_send = grad_query_blocks.reshape(seq_total, 1, heads_local, HD)
     grad_kv_send = jnp.stack([kv_grads[0], kv_grads[1]], axis=2).astype(jnp.bfloat16)
     grad_query_tok, grad_kv_tok = (
-        lax.all_to_all(grad_query_send, "seq", split_axis=0, concat_axis=1, tiled=True),
+        register_the_sides(grad_query_send),
         lax.all_to_all(grad_kv_send, "seq", split_axis=0, concat_axis=1, tiled=True),
     )
     grad_query_rot = grad_query_tok.reshape(tok_count, QH, HD).astype(jnp.float32)

time: 2950 us -> 2940 us (level)
    all_to_all x1, waiting for transfers between devices: 86.4 us -> 15 us  [per_device(): lax.all_to_all(grad_kv_send, 'seq', split_axis=0, concat_axis=1, tiled=True)]
    ppermute x0 -> x3, waiting for transfers between devices: none -> 49.2 us  [series_all_step_on(): jax.lax.ppermute(after, axis_key, [(m, (m + kk) % out_arr) for m in range...]
    reduce_scatter x1, waiting for transfers between devices: 278 us -> 311 us  [per_device(): lax.psum_scatter(grad_out_local, ('seq', 'fsdp'), scatter_dimension=0, ti...]
    all_to_all x1 -> x0, blocking collectives: 30.9 us -> none  [per_device(): lax.all_to_all(grad_kv_send, 'seq', split_axis=0, concat_axis=1, tiled=True)]
  transfers between devices with their start and end apart: 17 -> 20, of which waited for: 10 -> 13; matrix products, arithmetic and copies ran while one was open for 19% -> 19% of each run, Pallas kernels for 0% -> 0%
where the time goes in v1:
time: 2940 us
  waiting for transfers between devices  1810 us (62%)
  blocking collectives  390 us (13%)
  matrix products  288 us (10%)
  local copies, waits for them, and re-layouts  224 us (8%)
  other arithmetic  164 us (6%)
  starting transfers between devices  41.6 us (1%)
    reduce_scatter x1, waiting for transfers between devices, per_device(): lax.psum_scatter(grad_qkv_local, ('seq', 'fsdp'), scatter_dimension=0, ti...  454 us
    reduce_scatter x1, waiting for transfers between devices, per_device(): lax.psum_scatter(grad_out_local, ('seq', 'fsdp'), scatter_dimension=0, ti...  311 us
    all_gather x1, waiting for transfers between devices, expert_weights(): lax.all_gather(w_gate_up, 'seq', axis=1, tiled=True)  290 us
    all_gather x1, waiting for transfers between devices, expert_weights(): lax.all_gather(w_down, 'seq', axis=2, tiled=True)  184 us
    all_gather x1, blocking collectives, per_device(): lax.all_gather(w_router, ('seq', 'fsdp'), axis=0, tiled=True)  146 us
    all_to_all x1, blocking collectives, from_experts(): lax.all_to_all(rows, 'fsdp', split_axis=0, concat_axis=0, tiled=True)  126 us
    all_to_all x2, waiting for transfers between devices, to_experts(): lax.all_to_all(shaped, 'fsdp', split_axis=0, concat_axis=0, tiled=True)  121 us
    unnamed x2, blocking collectives  118 us
  transfers between devices with their start and end apart: 20, of which 13 were waited for; matrix products, arithmetic and copies ran while one was open for 19% of the time, Pallas kernels for 0%

profile of v1, /device:TPU:1, one launch (start us, length us, event | category | flops | bytes accessed | tf_op | source)
XLA Modules:
  0.0 2935.1 jit_solution(5869002714759756999)
XLA Ops:
  10.9 43.2 %all-reduce = bf16[4352]{0:T(1024)(128)(2,1)S(1)} all-reduce(bf16[4352]{0:T(1024)(128)(2,1)S(1)} %dynamic-update-slice), channel_id=1, replica_groups=mesh['seq'=4,'fsdp'=8] {'seq','fsdp'}, use_global_device_ids=true, to_apply=%add | all-reduce | flops 4352 | bytes 17408
  55.0 93.7 %all-gather.6.cloned.1.call-done = bf16[2048,5120]{1,0:T(8,128)(2,1)} async-done(((bf16[64,5120]{1,0:T(8,128)(2,1)}), bf16[2048,5120]{1,0:T(8,128)(2,1)}) %all-gather.6.cloned.1.call-update) | async-done | bytes 20971536 | tf_op jit(solution)/shard_map/all_gather | solution.py:107
  193.0 87.3 %all-to-all-done = bf16[256,4,8,128]{0,3,2,1:T(8,128)(2,1)S(1)} async-done(((bf16[256,4,8,128]{0,3,2,1:T(8,128)(2,1)}), bf16[256,4,8,128]{0,3,2,1:T(8,128)(2,1)S(1)}, u32[]{:S(2)}, u32[]{:S(2)}) %all-to-all-start) | async-done | bytes 2097184 | tf_op jit(solution)/shard_map/all_to_all | solution.py:141
  286.4 33.8 %while.30 = (s32[]{:T(128)}, bf16[2,512,1,8,128]{4,3,1,0,2:T(8,128)(2,1)}, f32[2,1,8,512]{3,2,1,0:T(8,128)S(1)}, s32[2]{0:T(128)S(1)}, s32[]{:T(128)}, /*index=5...) while((s32[]{:T(128)}, ...), condition=%wide.region_6.7_spmd.clone.clone, body=%wide.region_3.6_spmd.clone.clone.sunk | while | flops 2199385600 | bytes 57285240 | solution.py:178
  339.1 99.5 %all-to-all-done.2 = bf16[1024,1,8,128]{3,2,1,0:T(8,128)(2,1)} async-done(((bf16[1024,1,8,128]{3,2,1,0:T(8,128)(2,1)}), bf16[1024,1,8,128]{3,2,1,0:T(8,128)(2,1)}, u32[]{:S(2)}, u32[]{:S(2)}) %all-to-all-start.2) | async-done | bytes 2097184 | tf_op jit(solution)/shard_map/all_to_all | solution.py:180
  480.0 290.5 %all-gather.10.cloned.1.call-done = bf16[4,2048,1536]{2,1,0:T(8,128)(2,1)} async-done(((bf16[4,512,1536]{2,1,0:T(8,128)(2,1)}), bf16[4,2048,1536]{2,1,0:T(8,128)(2,1)}) %all-gather.10.cloned.1.call-update) | async-done | bytes 25165840 | tf_op jit(solution)/shard_map/all_gather | solution.py:88
  770.5 25.7 fusion.75
  804.3 184.0 %all-gather.12.cloned.1.call-done = bf16[4,768,2048]{2,1,0:T(8,128)(2,1)} async-done(((bf16[4,768,512]{2,1,0:T(8,128)(2,1)}), bf16[4,768,2048]{2,1,0:T(8,128)(2,1)}) %all-gather.12.cloned.1.call-update) | async-done | bytes 12582928 | tf_op jit(solution)/shard_map/all_gather | solution.py:89
  1021.0 145.7 %all-gather = bf16[32,64,32]{1,2,0:T(8,128)(2,1)S(1)} all-gather(bf16[1,64,32]{1,2,0:T(8,128)(2,1)S(1)} %bitcast.465), channel_id=1, replica_groups=mesh['seq'=4,'fsdp'=8] {'seq','fsdp'}, dimensions={0}, use_global_device_ids=true | all-gather | bytes 135168 | tf_op jit(solution)/shard_map/all_gather | solution.py:109
  1169.3 21.6 gather_fusion.3
  1201.4 24.6 gather_fusion.1
  1243.4 121.1 %all-to-all-done.5 = bf16[8,320,2048]{2,1,0:T(8,128)(2,1)} async-done(((bf16[8,320,2048]{2,1,0:T(8,128)(2,1)}), bf16[8,320,2048]{2,1,0:T(8,128)(2,1)}, u32[]{:S(2)}, u32[]{:S(2)}) %all-to-all-start.5) | async-done | bytes 10485792 | tf_op jit(solution)/shard_map/all_to_all | solution.py:78
  1408.5 27.1 bitcast_convert_fusion
  1435.8 23.6 convert_bitcast_fusion.1
  1469.5 125.7 %all_to_all.92 = bf16[8,320,2048]{2,1,0:T(8,128)(2,1)} all-to-all(bf16[8,320,2048]{2,1,0:T(8,128)(2,1)} %bitcast.435), channel_id=1, replica_groups=mesh['seq'=4,'fsdp'=8] {'fsdp'}, dimensions={0} | all-to-all | bytes 20971520 | tf_op jit(solution)/shard_map/all_to_all | solution.py:82
  1595.2 21.7 gather_fusion.4
  1651.2 18.6 fusion.106
  1678.8 103.2 %all-to-all-done.7 = bf16[256,4,8,128]{3,2,0,1:T(8,128)(2,1)S(1)} async-done(((bf16[256,4,8,128]{3,2,0,1:T(8,128)(2,1)}), bf16[256,4,8,128]{3,2,0,1:T(8,128)(2,1)S(1)}, u32[]{:S(2)}, u32[]{:S(2)}) %all-to-all-start.7) | async-done | bytes 2097184 | tf_op jit(solution)/shard_map/all_to_all | solution.py:285
  1783.6 91.2 %while.31 = (s32[]{:T(128)}, f32[1024,1,128]{0,2,1:T(8,128)}, f32[1024,1,128]{0,2,1:T(8,128)}, bf16[2,512,1,8,128]{4,3,1,0,2:T(8,128)(2,1)}, bf16[2,512,1,8,128]...) while((s32[]{:T(128)}, f32[1024,1,128]{0,2,1:T(8,128)}, ...), condition=%wide.region_20.22_spmd.clone.clone, body=%wide.region_18.21_spmd.clone.clone.sunk | while | flops 5409207808 | bytes 199187792 | solution.py:318
  1904.0 35.0 %collective-permute-done.1 = bf16[256,1,8,128]{3,2,0,1:T(8,128)(2,1)} collective-permute-done((bf16[256,1,8,128]{3,2,0,1:T(8,128)(2,1)S(1)}, bf16[256,1,8,128]{3,2,0,1:T(8,128)(2,1)}, u32[]{:S(2)}, u32[]{:S(2)}) %collective-permute-start.1) | collective-permute-done | bytes 524320 | tf_op jit(solution)/shard_map/ppermute | solution.py:41
  2012.7 18.6 fusion.107
  2069.0 75.3 %all-reduce.1 = f32[4352]{0:T(1024)S(1)} all-reduce(f32[4352]{0:T(1024)S(1)} %pad_maximum_fusion.9), channel_id=5, replica_groups=mesh['seq'=4,'fsdp'=8] {'seq','fsdp'}, use_global_device_ids=true, to_apply=%region_31.33.clone | all-reduce | flops 4352 | bytes 34816
  2163.3 310.7 %reduce-scatter.10.cloned.1.call-done = f32[128,2048]{1,0:T(8,128)} async-done(((f32[4096,2048]{1,0:T(8,128)}), f32[128,2048]{1,0:T(8,128)}) %reduce-scatter.10.cloned.1.call-update) | async-done | bytes 1048592 | tf_op jit(solution)/shard_map/reduce_scatter | solution.py:358
  2474.0 454.2 %reduce-scatter.8.cloned.1.call-done = f32[64,5120]{1,0:T(8,128)} async-done(((f32[2048,5120]{1,0:T(8,128)}), f32[64,5120]{1,0:T(8,128)}) %reduce-scatter.8.cloned.1.call-update) | async-done | bytes 1310736 | tf_op jit(solution)/shard_map/reduce_scatter | solution.py:357
  (402 shorter events, 568.1 us)
Async XLA Ops:
  7.2 141.5 %all-gather.6.cloned.1.call-start = ((), (), s32[]{:S(2)}) async-start(), calls=%async_computation.14 | async-start | bytes 21626880 | tf_op jit(solution)/shard_map/all_gather | solution.py:107
  7.9 435.0 %all-gather.8.cloned.1.call-start = ((), (), s32[]{:S(2)}) async-start(), calls=%async_computation.15 | async-start | bytes 17301504 | tf_op jit(solution)/shard_map/all_gather | solution.py:108
  8.7 761.8 %all-gather.10.cloned.1.call-start = ((), (), s32[]{:S(2)}) async-start(), calls=%async_computation.16 | async-start | bytes 31457280 | tf_op jit(solution)/shard_map/all_gather | solution.py:88
  10.4 175.6 %copy-start.36 = (f32[256,64]{0,1:T(8,128)}, f32[256,64]{0,1:T(8,128)S(1)}, u32[]{:S(2)}) copy-start(f32[256,64]{0,1:T(8,128)S(1)} %get-tuple-element.498) | copy-start | bytes 196612
  10.5 151.6 %copy-start.32 = (f32[256,64]{1,0:T(8,128)}, f32[256,64]{1,0:T(8,128)S(1)}, u32[]{:S(2)}) copy-start(f32[256,64]{1,0:T(8,128)S(1)} %copy.364) | copy-start | bytes 196612
  54.4 128.7 %copy-start.68 = (f32[128]{0:T(128)}, f32[128]{0:T(128)S(1)}, u32[]{:S(2)}) copy-start(f32[128]{0:T(128)S(1)} %get-tuple-element.495) | copy-start | bytes 1540
  163.4 24.8 all-to-all-start.1
  188.2 92.1 %all-to-all-start = ((bf16[256,4,8,128]{0,3,2,1:T(8,128)(2,1)}), bf16[256,4,8,128]{0,3,2,1:T(8,128)(2,1)S(1)}, u32[]{:S(2)}, u32[]{:S(2)}) async-start(bf16[256,4,8,128]{0,3,2,1:T(8,128)(2,1)} %pad_maximum_fusion.3), calls=%async_computation | async-start | bytes 4194304 | tf_op jit(solution)/shard_map/all_to_all | solution.py:141
  321.0 117.6 %all-to-all-start.2 = ((bf16[1024,1,8,128]{3,2,1,0:T(8,128)(2,1)}), bf16[1024,1,8,128]{3,2,1,0:T(8,128)(2,1)}, u32[]{:S(2)}, u32[]{:S(2)}) async-start(bf16[1024,1,8,128]{3,2,1,0:T(8,128)(2,1)} %bitcast.17), calls=%async_computation.2 | async-start | bytes 4194304 | tf_op jit(solution)/shard_map/all_to_all | solution.py:180
  325.5 662.8 %all-gather.12.cloned.1.call-start = ((), (), s32[]{:S(2)}) async-start(), calls=%async_computation.17 | async-start | bytes 15728640 | tf_op jit(solution)/shard_map/all_gather | solution.py:89
  474.1 296.5 %all-to-all-start.3 = ((bf16[8,320,2048]{2,1,0:T(8,128)(2,1)}), bf16[8,320,2048]{2,1,0:T(8,128)(2,1)}, u32[]{:S(2)}, u32[]{:S(2)}) async-start(bf16[8,320,2048]{2,1,0:T(8,128)(2,1)} %broadcast_select_fusion.1), calls=%async_computation.3 | async-start | bytes 20971520 | tf_op jit(solution)/shard_map/all_to_all | solution.py:78
  1014.5 154.7 %all-to-all-start.4 = ((bf16[8,320,2048]{2,1,0:T(8,128)(2,1)}), bf16[8,320,2048]{2,1,0:T(8,128)(2,1)}, u32[]{:S(2)}, u32[]{:S(2)}) async-start(bf16[8,320,2048]{2,1,0:T(8,128)(2,1)} %bitcast.432), calls=%async_computation.4 | async-start | bytes 20971520 | tf_op jit(solution)/shard_map/all_to_all | solution.py:82
  1020.2 148.9 %copy-start.54 = (s32[1,256,8]{1,2,0:T(8,128)S(1)}, s32[1,256,8]{1,2,0:T(8,128)}, u32[]{:S(2)}) copy-start(s32[1,256,8]{1,2,0:T(8,128)} %param.20) | copy-start | bytes 24580
  1236.0 128.6 %all-to-all-start.5 = ((bf16[8,320,2048]{2,1,0:T(8,128)(2,1)}), bf16[8,320,2048]{2,1,0:T(8,128)(2,1)}, u32[]{:S(2)}, u32[]{:S(2)}) async-start(bf16[8,320,2048]{2,1,0:T(8,128)(2,1)} %broadcast_select_fusion), calls=%async_computation.5 | async-start | bytes 20971520 | tf_op jit(solution)/shard_map/all_to_all | solution.py:78
  1241.2 797.2 %reduce-scatter.16.cloned.1.call-start = ((), (), s32[]{:S(2)}) async-start(), calls=%async_computation.22 | async-start | bytes 1081344
  1243.4 905.0 %reduce-scatter.14.cloned.1.call-start = ((), (), s32[]{:S(2)}) async-start(), calls=%async_computation.21 | async-start | bytes 15728640 | tf_op jit(solution)/shard_map/reduce_scatter | solution.py:259
  1381.2 772.8 %reduce-scatter.12.cloned.1.call-start = ((), (), s32[]{:S(2)}) async-start(), calls=%async_computation.20 | async-start | bytes 31457280 | tf_op jit(solution)/shard_map/reduce_scatter | solution.py:256
  1435.6 1038.4 %reduce-scatter.10.cloned.1.call-start = ((), (), s32[]{:S(2)}) async-start(), calls=%async_computation.19 | async-start | bytes 34603008 | tf_op jit(solution)/shard_map/reduce_scatter | solution.py:358
  1673.6 108.4 %all-to-all-start.7 = ((bf16[256,4,8,128]{3,2,0,1:T(8,128)(2,1)}), bf16[256,4,8,128]{3,2,0,1:T(8,128)(2,1)S(1)}, u32[]{:S(2)}, u32[]{:S(2)}) async-start(bf16[256,4,8,128]{3,2,0,1:T(8,128)(2,1)} %copy.384), calls=%async_computation.7 | async-start | bytes 4194304 | tf_op jit(solution)/shard_map/all_to_all | solution.py:285
  1877.4 26.6 collective-permute-start
  1877.4 61.6 %collective-permute-start.1 = (bf16[256,1,8,128]{3,2,0,1:T(8,128)(2,1)S(1)}, bf16[256,1,8,128]{3,2,0,1:T(8,128)(2,1)}, u32[]{:S(2)}, u32[]{:S(2)}) collective-permute-start(bf16[256,1,8,128]{3,2,0,1:T(8,128)(2,1)S(1)} %get-tuple-element.479), channel_id=1, source_target_pairs={{0,16},{8,24},{16,0},{24,8},{1,17},{9,25},{17,1},{25,9},{2,18},{10... | collective-permute-start | bytes 1572872 | tf_op jit(solution)/shard_map/ppermute | solution.py:41
  1877.4 67.7 %collective-permute-start.2 = (bf16[256,1,8,128]{3,2,0,1:T(8,128)(2,1)S(1)}, bf16[256,1,8,128]{3,2,0,1:T(8,128)(2,1)}, u32[]{:S(2)}, u32[]{:S(2)}) collective-permute-start(bf16[256,1,8,128]{3,2,0,1:T(8,128)(2,1)S(1)} %get-tuple-element.478), channel_id=1, source_target_pairs={{0,24},{8,0},{16,8},{24,16},{1,25},{9,1},{17,9},{25,17},{2,26},{10... | collective-permute-start | bytes 1572872 | tf_op jit(solution)/shard_map/ppermute | solution.py:41
  1891.7 111.7 %all-to-all-start.8 = ((bf16[1024,1,2,128]{3,2,1,0:T(2,128)(2,1)}), bf16[1024,1,2,128]{3,2,1,0:T(2,128)(2,1)}, u32[]{:S(2)}, u32[]{:S(2)}) async-start(bf16[1024,1,2,128]{3,2,1,0:T(2,128)(2,1)} %copy.396), calls=%async_computation.8 | async-start | bytes 1048576 | tf_op jit(solution)/shard_map/all_to_all | solution.py:325
  1895.8 1032.4 %reduce-scatter.8.cloned.1.call-start = ((), (), s32[]{:S(2)}) async-start(), calls=%async_computation.18 | async-start | bytes 43253760 | tf_op jit(solution)/shard_map/reduce_scatter | solution.py:357
  (79 other events, 1553.9 us)
Sparse Core Ops, SparseCore 0:
  10.9 137.8 all-gather.5
  151.6 149.4 all-gather.7
  302.7 467.7 all-gather.9
  771.9 216.3 all-gather.11
  1243.9 132.2 reduce-scatter.15
  1381.3 211.4 reduce-scatter.13
  1595.2 506.0 reduce-scatter.11
  2104.1 369.8 reduce-scatter.9
  2476.9 451.2 reduce-scatter.7
